TPU v7x, 32 devices: a whole 2x2x4 slice. The times are simulated.
32 devices in a mesh: row: 16 (over z, y, x), col: 2 (over core).
Axes of the slice: x: 2, y: 2, z: 4, core: 2. Of those that a mesh axis runs over, the one named last changes fastest.
Arguments:
- orbitals: float32 [3072, 512], P(('row', 'col')), may hold values from -6 to 6
- coulomb: float32 [3072, 2, 1536], P('row', 'col'), may hold values from -0.00478416 to 0.00478416, as said below
Outputs:
- exchange: float32 [3072, 512], P(('row', 'col'))
Inputs may be any that keep to these rules, and one draw needn't show every extreme that they name: V built from coulomb is symmetric.
All inputs are finite; a program needn't handle non-finite values.
Results may differ from a plain program's by a relative error of at most 0.0001.
Values sent between devices are 32-bit elements; how exact they have to be, the bound alone decides.
No kernel may reach another device: no remote copies, remote signals or barrier semaphores. Data moves between devices by JAX's collectives and lax.ppermute only.
A program may use at most 64 MiB of HBM per device.

v0:
```python
import jax
import jax.numpy as jnp
from jax import lax
from jax.sharding import PartitionSpec as P


def body(orbitals, coulomb):
    row_panel = lax.all_gather(orbitals, "col", axis=0, tiled=True)
    row_count = row_panel.shape[0]
    kernel_tile = coulomb.reshape(row_count, -1)
    pieces = lax.all_gather(orbitals, "row", axis=0, tiled=True)
    gram_piece = lax.dot_general(
        row_panel,
        pieces,
        (((1,), (1,)), ((), ())),
        precision=lax.Precision.HIGHEST,
        preferred_element_type=jnp.float32,
    )
    partial_value = jnp.dot(
        gram_piece * kernel_tile,
        pieces,
        precision=lax.Precision.HIGHEST,
        preferred_element_type=jnp.float32,
    )
    return lax.psum_scatter(partial_value, "col", scatter_dimension=0, tiled=True)


def solution(mesh):
    placed = (P(("row", "col"), None), P("row", "col", None))
    return jax.shard_map(
        body, mesh=mesh, in_specs=placed, out_specs=P(("row", "col"), None), check_vma=False
    )
```

profile of v0, /device:TPU:0, one launch (start us, length us, event | category | flops | bytes accessed | tf_op | source)
XLA Modules:
  0.0 102.8 jit_solution(13407295416819787636)
XLA Ops:
  6.5 0.0 all-gather.2.cloned.1.call-start
  6.5 0.7 all-gather.2.cloned.1.call-update
  7.3 0.0 reduce-scatter.2.cloned.1.call-start
  7.3 2.4 %all_gather.6 = f32[192,512]{1,0:T(8,128)S(1)} all-gather(f32[96,512]{1,0:T(8,128)} %param.2), channel_id=1, replica_groups=mesh['row'=16,'col'=2] {'col'}, dimensions={0}, use_global_device_ids=true | all-gather | bytes 589824 | tf_op jit(solution)/shard_map/all_gather | solution.py:8
  9.7 71.0 %all-gather.2.cloned.1.call-done = f32[1536,512]{1,0:T(8,128)} async-done(((f32[96,512]{1,0:T(8,128)}), f32[1536,512]{1,0:T(8,128)}) %all-gather.2.cloned.1.call-update) | async-done | bytes 3145744 | tf_op jit(solution)/shard_map/all_gather | solution.py:11
  80.7 0.0 copy-start
  80.7 5.7 %convolution_multiply_fusion = f32[192,1536]{1,0:T(8,128)S(1)} fusion(f32[192,512]{1,0:T(8,128)S(1)} %all_gather.6, f32[1536,512]{1,0:T(8,128)} %all-gather.2.cloned.1.call-done, f32[192,1,1536]{2,1,0:T(1,128)} %param.3), kind=kOutput, calls=%fused_computation | convolution fusion | flops 1812234240 | bytes 5898240 | tf_op jit(solution)/shard_map/dot_general | solution.py:12
  86.4 0.0 copy-done
  86.4 3.0 %fusion = f32[192,512]{1,0:T(8,128)} fusion(f32[192,1536]{1,0:T(8,128)S(1)} %convolution_multiply_fusion, f32[1536,512]{1,0:T(8,128)S(1)} %copy-done), kind=kOutput, calls=%fused_computation.1 | convolution fusion | flops 1811939328 | bytes 4718592 | tf_op jit(solution)/shard_map/dot_general | solution.py:19
  89.5 0.0 reduce-scatter.2.cloned.1.call-update
  89.5 6.5 %reduce-scatter.2.cloned.1.call-done = f32[96,512]{1,0:T(8,128)} async-done(((f32[192,512]{1,0:T(8,128)}), f32[96,512]{1,0:T(8,128)}) %reduce-scatter.2.cloned.1.call-update) | async-done | bytes 196624 | tf_op jit(solution)/shard_map/reduce_scatter | solution.py:25
Async XLA Ops:
  6.5 74.2 %all-gather.2.cloned.1.call-start = ((), (), s32[]{:S(2)}) async-start(), calls=%async_computation.1 | async-start | bytes 3342336 | tf_op jit(solution)/shard_map/all_gather | solution.py:11
  7.3 88.7 %reduce-scatter.2.cloned.1.call-start = ((), (), s32[]{:S(2)}) async-start(), calls=%async_computation.2 | async-start | bytes 589824 | tf_op jit(solution)/shard_map/reduce_scatter | solution.py:25
  80.7 5.7 %copy-start = (f32[1536,512]{1,0:T(8,128)S(1)}, f32[1536,512]{1,0:T(8,128)}, u32[]{:S(2)}) copy-start(f32[1536,512]{1,0:T(8,128)} %all-gather.2.cloned.1.call-done) | copy-start | bytes 9437188
Sparse Core Ops, SparseCore 0:
  10.1 70.5 all-gather.1
  89.6 6.3 reduce-scatter.1
where the time goes:
time: 103 us
  waiting for transfers between devices  78.2 us (76%)
  between operations  13.4 us (13%)
  matrix products  8.71 us (8%)
  blocking collectives  2.42 us (2%)
    all_gather x1, waiting for transfers between devices, body(): pieces = lax.all_gather(orbitals, 'row', axis=0, tiled=True)  71 us
    reduce_scatter x1, waiting for transfers between devices, body(): lax.psum_scatter(partial_value, 'col', scatter_dimension=0, tiled=True)  6.51 us
    dot_general x1, matrix products, body(): lax.dot_general(row_panel, pieces, (((1,), (1,)), ((), ())), precision=la...  5.7 us
    dot_general x1, matrix products, body(): jnp.dot(gram_piece * kernel_tile, pieces, precision=lax.Precision.HIGHEST...  3.02 us
    all_gather x1, blocking collectives, body(): row_panel = lax.all_gather(orbitals, 'col', axis=0, tiled=True)  2.42 us
  transfers between devices with their start and end apart: 2, of which 2 were waited for; matrix products, arithmetic and copies ran while one was open for 0% of the time, Pallas kernels for 0%

commit v1 on v0

v1 whole, which is shorter than its diff:
```python
import functools

import jax
import jax.numpy as jnp
from jax import lax
from jax.experimental import pallas as pl
from jax.experimental.pallas import tpu as pltpu
from jax.sharding import PartitionSpec as P

AXES = ("row", "col")
NT = (((1,), (1,)), ((), ()))
TN = (((0,), (0,)), ((), ()))


def split(x):
    high = x.astype(jnp.bfloat16)
    return high, (x - high.astype(jnp.float32)).astype(jnp.bfloat16)


def product(a, b, dims):
    dot = functools.partial(lax.dot_general, dimension_numbers=dims, preferred_element_type=jnp.float32)
    return dot(a[0], b[0]) + (dot(a[0], b[1]) + dot(a[1], b[0]))


def tile_kernel(n_panel, n_block, first, *refs):
    refs = list(refs)
    take = lambda n: [refs.pop(0) for _ in range(n)]
    (where,), panel, blocks, (kernel_t,) = take(1), take(n_panel), take(n_block), take(1)
    totals_in = [] if first else take(n_panel)
    totals = take(n_panel)
    points = blocks[0].shape[0]
    rows = split(jnp.concatenate([p[...] for p in panel], axis=0))
    columns = split(jnp.concatenate([b[...] for b in blocks], axis=0))
    coulomb = jnp.concatenate(
        [kernel_t[pl.ds(pl.multiple_of(where[i] * points, points), points), :] for i in range(n_block)], axis=0
    )
    tile = split(product(columns, rows, NT) * coulomb)
    result = product(tile, columns, TN)
    for i in range(n_panel):
        piece = result[i * points : (i + 1) * points]
        totals[i][...] = piece if first else totals_in[i][...] + piece


def add_tile(where, panel, blocks, kernel_t, totals):
    points, orbitals = blocks[0].shape
    n_panel, n_block, first = len(panel), len(blocks), totals is None
    rows, columns = n_panel * points, n_block * points
    operands = [where, *panel, *blocks, kernel_t] + ([] if first else list(totals))
    vmem = pl.BlockSpec(memory_space=pltpu.VMEM)
    return pl.pallas_call(
        functools.partial(tile_kernel, n_panel, n_block, first),
        out_shape=[jax.ShapeDtypeStruct((points, orbitals), jnp.float32)] * n_panel,
        in_specs=[pl.BlockSpec(memory_space=pltpu.SMEM)] + [vmem] * (len(operands) - 1),
        out_specs=[vmem] * n_panel,
        cost_estimate=pl.CostEstimate(
            flops=12 * rows * columns * orbitals, bytes_accessed=4 * (rows + columns) * orbitals, transcendentals=0
        ),
        compiler_params=pltpu.CompilerParams(vmem_limit_bytes=24 << 20),
        name="add_tile",
    )(*operands)


def solution(mesh):
    n_row, n_col = mesh.shape["row"], mesh.shape["col"]

    def move(x, target):
        pairs = []
        for r in range(n_row):
            for c in range(n_col):
                r2, c2 = target(r, c)
                pairs.append((r * n_col + c, r2 * n_col + c2))
        return lax.ppermute(x, AXES, pairs)

    def hop(x, even, odd):
        return move(x, lambda r, c: (r ^ (odd if c % 2 else even), c))

    def turn(x, k):
        return move(x, lambda r, c: (r, (c + k) % n_col))

    def body(orbitals, coulomb):
        row, col = lax.axis_index("row"), lax.axis_index("col")
        points = orbitals.shape[0]
        panel = [orbitals] + [turn(orbitals, -k) for k in range(1, n_col)]
        tile = coulomb.reshape(n_col * points, n_row * points)
        kernel_t = jnp.concatenate(
            [lax.dynamic_slice_in_dim(tile, (col + k) % n_col * points, points, 0).T for k in range(n_col)], axis=1
        )
        odd = col % 2
        first_step, second_step = 1 + odd, 2 - odd
        totals = None
        slots = [(orbitals, 0)] + [(hop(orbitals, far, far), far) for far in range(4, n_row, 4)]
        for block, far in slots:
            first = hop(block, 1, 2)
            second = hop(block, 2, 1)
            third = hop(first, 2, 1)
            base = row ^ far
            where = jnp.stack([base, base ^ first_step, base ^ second_step, base ^ 3]).astype(jnp.int32)
            totals = add_tile(where, panel, [block, first, second, third], kernel_t, totals)
        result = totals[0]
        for k in range(1, n_col):
            result = result + turn(totals[k], k)
        return result

    placed = (P(("row", "col"), None), P("row", "col", None))
    return jax.shard_map(body, mesh=mesh, in_specs=placed, out_specs=P(("row", "col"), None), check_vma=False)
```

time: 103 us -> 46.4 us (0.45)
  waiting for transfers between devices: 78.2 us -> 12.6 us
  starting transfers between devices: 0.04 us -> 17.1 us
  between operations: 13.4 us -> 0.12 us
  Pallas kernels: 0 us -> 9.06 us
  matrix products: 8.71 us -> 0 us
  local copies, waits for them, and re-layouts: 0.01 us -> 4.42 us
  other arithmetic: 0 us -> 2.85 us
  blocking collectives: 2.42 us -> 0 us
    all_gather x1 -> x0, waiting for transfers between devices: 71 us -> none  [body(): pieces = lax.all_gather(orbitals, 'row', axis=0, tiled=True)]
    ppermute x0 -> x17, starting transfers between devices: none -> 17.1 us  [move(): return lax.ppermute(x, AXES, pairs)]
    ppermute x0 -> x17, waiting for transfers between devices: none -> 12.6 us  [move(): return lax.ppermute(x, AXES, pairs)]
    pallas_call x0 -> x4, Pallas kernels: none -> 9.06 us  [add_tile(): pl.pallas_call(functools.partial(tile_kernel, n_panel, n_block, first), o...]
    dot_general x2 -> x0, matrix products: 8.71 us -> none  [the longest x1 5.7 us: body(): lax.dot_general(row_panel, pieces, (((1,), (1,)), ((), ())), precision=la...]
    reduce_scatter x1 -> x0, waiting for transfers between devices: 6.51 us -> none  [body(): lax.psum_scatter(partial_value, 'col', scatter_dimension=0, tiled=True)]
    dynamic_slice x0 -> x3, local copies, waits for them, and re-layouts: none -> 4.42 us  [body(): lax.dynamic_slice_in_dim(tile, (col + k) % n_col * points, points, 0)]
    all_gather x1 -> x0, blocking collectives: 2.42 us -> none  [body(): row_panel = lax.all_gather(orbitals, 'col', axis=0, tiled=True)]
  transfers between devices with their start and end apart: 2 -> 17, of which waited for: 2 -> 6; matrix products, arithmetic and copies ran while one was open for 0% -> 14% of each run, Pallas kernels for 0% -> 15%
where the time goes in v1:
time: 46.4 us; the launch traced here: 46.2 us
  starting transfers between devices  17.1 us (37%)
  waiting for transfers between devices  12.6 us (27%)
  Pallas kernels  9.06 us (20%)
  local copies, waits for them, and re-layouts  4.42 us (10%)
  other arithmetic  2.85 us (6%)
    ppermute x17, starting transfers between devices, move(): return lax.ppermute(x, AXES, pairs)  17.1 us
    ppermute x17, waiting for transfers between devices, move(): return lax.ppermute(x, AXES, pairs)  12.6 us
    pallas_call x4, Pallas kernels, add_tile(): pl.pallas_call(functools.partial(tile_kernel, n_panel, n_block, first), o...  9.06 us
    dynamic_slice x3, local copies, waits for them, and re-layouts, body(): lax.dynamic_slice_in_dim(tile, (col + k) % n_col * points, points, 0)  4.42 us
    concatenate x1, other arithmetic, body(): jnp.concatenate([lax.dynamic_slice_in_dim(tile, (col + k) % n_col * point...  1.84 us
  transfers between devices with their start and end apart: 17, of which 6 were waited for; matrix products, arithmetic and copies ran while one was open for 14% of the time, Pallas kernels for 15%

profile of v1, /device:TPU:0, one launch (start us, length us, event | category | flops | bytes accessed | tf_op | source)
XLA Modules:
  0.0 46.2 jit_solution(362655998774539341)
XLA Ops:
  0.0 0.5 %collective-permute-start = (f32[96,512]{1,0:T(8,128)}, f32[96,512]{1,0:T(8,128)S(1)}, u32[]{:S(2)}, u32[]{:S(2)}) collective-permute-start(f32[96,512]{1,0:T(8,128)} %refs_1_.7), channel_id=1, source_target_pairs={{0,1},{1,0},{2,3},{3,2},{4,5},{5,4},{6,7},{7,6},{8,9},{9,8},{10,11... | collective-permute-start | bytes 589832 | tf_op jit(solution)/shard_map/ppermute | solution.py:72
  0.5 2.5 %collective-permute-start.13 = (f32[96,512]{1,0:T(8,128)}, f32[96,512]{1,0:T(8,128)S(1)}, u32[]{:S(2)}, u32[]{:S(2)}) collective-permute-start(f32[96,512]{1,0:T(8,128)} %refs_1_.7), channel_id=1, source_target_pairs={{0,2},{1,5},{2,0},{3,7},{4,6},{5,1},{6,4},{7,3},{8,10},{9,13},{10,... | collective-permute-start | bytes 589832 | tf_op jit(solution)/shard_map/ppermute | solution.py:72
  3.0 1.5 %collective-permute-start.14 = (f32[96,512]{1,0:T(8,128)}, f32[96,512]{1,0:T(8,128)S(1)}, u32[]{:S(2)}, u32[]{:S(2)}) collective-permute-start(f32[96,512]{1,0:T(8,128)} %refs_1_.7), channel_id=1, source_target_pairs={{0,4},{1,3},{2,6},{3,1},{4,0},{5,7},{6,2},{7,5},{8,12},{9,11},{10,... | collective-permute-start | bytes 589832 | tf_op jit(solution)/shard_map/ppermute | solution.py:72
  4.5 1.6 %collective-permute-start.9 = (f32[96,512]{1,0:T(8,128)}, f32[96,512]{1,0:T(8,128)S(1)}, u32[]{:S(2)}, u32[]{:S(2)}) collective-permute-start(f32[96,512]{1,0:T(8,128)} %refs_1_.7), channel_id=1, source_target_pairs={{0,8},{1,9},{2,10},{3,11},{4,12},{5,13},{6,14},{7,15},{8,0},{9,1},... | collective-permute-start | bytes 589832 | tf_op jit(solution)/shard_map/ppermute | solution.py:72
  6.1 2.6 %collective-permute-start.5 = (f32[96,512]{1,0:T(8,128)}, f32[96,512]{1,0:T(8,128)S(1)}, u32[]{:S(2)}, u32[]{:S(2)}) collective-permute-start(f32[96,512]{1,0:T(8,128)} %refs_1_.7), channel_id=1, source_target_pairs={{0,16},{1,17},{2,18},{3,19},{4,20},{5,21},{6,22},{7,23},{8,24},{9,... | collective-permute-start | bytes 589832 | tf_op jit(solution)/shard_map/ppermute | solution.py:72
  8.7 2.1 %constant_dynamic-slice_fusion.1 = (f32[96,1,1536]{2,1,0:T(1,128)S(1)}, f32[96,1,1536]{2,1,0:T(1,128)S(1)}) fusion(f32[192,1,1536]{2,1,0:T(1,128)} %param.3, s32[]{:T(128)S(6)} %select_n.20, s32[]{:T(128)S(6)} %select_n.22), kind=kLoop, calls=%fused_computation.6 | loop fusion | bytes 2359304 | tf_op jit(solution)/shard_map/dynamic_slice | solution.py:86
  10.7 0.0 copy-start
  10.7 1.2 %copy.3 = f32[96,1,1536]{0,2,1:T(8,128)} copy(f32[96,1,1536]{2,1,0:T(1,128)S(1)} %get-tuple-element.21) | data formatting | bytes 1179648 | tf_op jit(solution)/shard_map/dynamic_slice | solution.py:86
  11.9 1.2 %copy.4 = f32[96,1,1536]{0,2,1:T(8,128)} copy(f32[96,1,1536]{2,1,0:T(1,128)S(1)} %get-tuple-element.22) | data formatting | bytes 1179648 | tf_op jit(solution)/shard_map/dynamic_slice | solution.py:86
  13.1 0.0 collective-permute-done.refs_2_
  13.1 0.2 collective-permute-start.1
  13.3 1.8 %pad_maximum_fusion.refs_7_ = f32[1536,192]{1,0:T(8,128)S(1)} fusion(f32[1536,96]{1,0:T(8,128)} %bitcast.23, f32[1536,96]{1,0:T(8,128)} %bitcast.22), kind=kLoop, calls=%fused_computation | loop fusion | flops 294912 | bytes 2359296 | tf_op jit(solution)/shard_map/concatenate | solution.py:85
  15.2 0.4 collective-permute-done.9.refs_3_
  15.5 0.5 %collective-permute-start.10 = (f32[96,512]{1,0:T(8,128)S(1)}, f32[96,512]{1,0:T(8,128)S(1)}, u32[]{:S(2)}, u32[]{:S(2)}) collective-permute-start(f32[96,512]{1,0:T(8,128)S(1)} %collective-permute-done.9.refs_3_), channel_id=1, source_target_pairs={{0,2},{1,5},{2,0},{3,7},{4,6},{5,1},{6,4},{7,3},{8,10},{9,13},{10,... | collective-permute-start | bytes 589832 | tf_op jit(solution)/shard_map/ppermute | solution.py:72
  16.1 0.1 pad_add_fusion.3.refs_0_
  16.1 0.0 collective-permute-done.13.refs_4_
  16.2 0.4 collective-permute-start.11
  16.5 0.0 collective-permute-done.14.refs_5_
  16.5 1.7 %collective-permute-start.15 = (f32[96,512]{1,0:T(8,128)S(1)}, f32[96,512]{1,0:T(8,128)S(1)}, u32[]{:S(2)}, u32[]{:S(2)}) collective-permute-start(f32[96,512]{1,0:T(8,128)S(1)} %collective-permute-done.13.refs_4_), channel_id=1, source_target_pairs={{0,4},{1,3},{2,6},{3,1},{4,0},{5,7},{6,2},{7,5},{8,12},{9,11},{10,... | collective-permute-start | bytes 589832 | tf_op jit(solution)/shard_map/ppermute | solution.py:72
  18.2 4.1 %collective-permute-done.5.refs_3_ = f32[96,512]{1,0:T(8,128)S(1)} collective-permute-done((f32[96,512]{1,0:T(8,128)}, f32[96,512]{1,0:T(8,128)S(1)}, u32[]{:S(2)}, u32[]{:S(2)}) %collective-permute-start.5) | collective-permute-done | bytes 196640 | tf_op jit(solution)/shard_map/ppermute | solution.py:72
  22.3 0.5 %collective-permute-start.6 = (f32[96,512]{1,0:T(8,128)S(1)}, f32[96,512]{1,0:T(8,128)}, u32[]{:S(2)}, u32[]{:S(2)}) collective-permute-start(f32[96,512]{1,0:T(8,128)S(1)} %collective-permute-done.5.refs_3_), channel_id=1, source_target_pairs={{0,2},{1,5},{2,0},{3,7},{4,6},{5,1},{6,4},{7,3},{8,10},{9,13},{10,... | collective-permute-start | bytes 589832 | tf_op jit(solution)/shard_map/ppermute | solution.py:72
  22.8 0.0 collective-permute-done.1.refs_3_
  22.8 1.5 %collective-permute-start.2 = (f32[96,512]{1,0:T(8,128)S(1)}, f32[96,512]{1,0:T(8,128)S(1)}, u32[]{:S(2)}, u32[]{:S(2)}) collective-permute-start(f32[96,512]{1,0:T(8,128)S(1)} %collective-permute-done.1.refs_3_), channel_id=1, source_target_pairs={{0,2},{1,5},{2,0},{3,7},{4,6},{5,1},{6,4},{7,3},{8,10},{9,13},{10,... | collective-permute-start | bytes 589832 | tf_op jit(solution)/shard_map/ppermute | solution.py:72
  24.3 0.1 pad_add_fusion.2.refs_0_
  24.4 0.0 collective-permute-done.10.refs_4_
  24.4 0.5 %collective-permute-start.12 = (f32[96,512]{1,0:T(8,128)S(1)}, f32[96,512]{1,0:T(8,128)}, u32[]{:S(2)}, u32[]{:S(2)}) collective-permute-start(f32[96,512]{1,0:T(8,128)S(1)} %collective-permute-done.10.refs_4_), channel_id=1, source_target_pairs={{0,4},{1,3},{2,6},{3,1},{4,0},{5,7},{6,2},{7,5},{8,12},{9,11},{10,... | collective-permute-start | bytes 589832 | tf_op jit(solution)/shard_map/ppermute | solution.py:72
  24.9 0.1 pad_add_fusion.1.refs_0_
  25.0 2.1 %collective-permute-done.15.refs_6_ = f32[96,512]{1,0:T(8,128)S(1)} collective-permute-done((f32[96,512]{1,0:T(8,128)S(1)}, f32[96,512]{1,0:T(8,128)S(1)}, u32[]{:S(2)}, u32[]{:S(2)}) %collective-permute-start.15) | collective-permute-done | bytes 196640 | tf_op jit(solution)/shard_map/ppermute | solution.py:72
  27.1 1.2 %collective-permute-start.7 = (f32[96,512]{1,0:T(8,128)S(1)}, f32[96,512]{1,0:T(8,128)S(1)}, u32[]{:S(2)}, u32[]{:S(2)}) collective-permute-start(f32[96,512]{1,0:T(8,128)S(1)} %collective-permute-done.5.refs_3_), channel_id=1, source_target_pairs={{0,4},{1,3},{2,6},{3,1},{4,0},{5,7},{6,2},{7,5},{8,12},{9,11},{10,... | collective-permute-start | bytes 589832 | tf_op jit(solution)/shard_map/ppermute | solution.py:72
  28.3 0.0 collective-permute-done.11.refs_5_
  28.3 0.8 %collective-permute-start.3 = (f32[96,512]{1,0:T(8,128)S(1)}, f32[96,512]{1,0:T(8,128)S(1)}, u32[]{:S(2)}, u32[]{:S(2)}) collective-permute-start(f32[96,512]{1,0:T(8,128)S(1)} %collective-permute-done.1.refs_3_), channel_id=1, source_target_pairs={{0,4},{1,3},{2,6},{3,1},{4,0},{5,7},{6,2},{7,5},{8,12},{9,11},{10,... | collective-permute-start | bytes 589832 | tf_op jit(solution)/shard_map/ppermute | solution.py:72
  29.1 1.0 %collective-permute-done.6.refs_4_ = f32[96,512]{1,0:T(8,128)} collective-permute-done((f32[96,512]{1,0:T(8,128)S(1)}, f32[96,512]{1,0:T(8,128)}, u32[]{:S(2)}, u32[]{:S(2)}) %collective-permute-start.6) | collective-permute-done | bytes 196640 | tf_op jit(solution)/shard_map/ppermute | solution.py:72
  30.2 0.5 %collective-permute-start.8 = (f32[96,512]{1,0:T(8,128)}, f32[96,512]{1,0:T(8,128)S(1)}, u32[]{:S(2)}, u32[]{:S(2)}) collective-permute-start(f32[96,512]{1,0:T(8,128)} %collective-permute-done.6.refs_4_), channel_id=1, source_target_pairs={{0,4},{1,3},{2,6},{3,1},{4,0},{5,7},{6,2},{7,5},{8,12},{9,11},{10,... | collective-permute-start | bytes 589832 | tf_op jit(solution)/shard_map/ppermute | solution.py:72
  30.7 3.6 %collective-permute-done.2.refs_4_ = f32[96,512]{1,0:T(8,128)S(1)} collective-permute-done((f32[96,512]{1,0:T(8,128)S(1)}, f32[96,512]{1,0:T(8,128)S(1)}, u32[]{:S(2)}, u32[]{:S(2)}) %collective-permute-start.2) | collective-permute-done | bytes 196640 | tf_op jit(solution)/shard_map/ppermute | solution.py:72
  34.3 0.5 %collective-permute-start.4 = (f32[96,512]{1,0:T(8,128)S(1)}, f32[96,512]{1,0:T(8,128)S(1)}, u32[]{:S(2)}, u32[]{:S(2)}) collective-permute-start(f32[96,512]{1,0:T(8,128)S(1)} %collective-permute-done.2.refs_4_), channel_id=1, source_target_pairs={{0,4},{1,3},{2,6},{3,1},{4,0},{5,7},{6,2},{7,5},{8,12},{9,11},{10,... | collective-permute-start | bytes 589832 | tf_op jit(solution)/shard_map/ppermute | solution.py:72
  34.8 0.1 pad_add_fusion.refs_0_
  34.8 2.0 %add_tile.4 = (f32[96,512]{1,0:T(8,128)S(1)}, f32[96,512]{1,0:T(8,128)S(1)}) custom-call(s32[4]{0:T(128)S(1)} %pad_add_fusion.3.refs_0_, f32[96,512]{1,0:T(8,128)S(1)} %copy-done, f32[96,512]{1,0:T(8,128)S(1)} %collective-permute-done.refs_2_, f32[96,512]{1,0:T(8,128)S(1)} %copy-done, f32[96,512]{1,0:T(8,128)S(1)} %collective-permute-done.13.refs_4_, ...), custom_call_target="tpu_custom_call" | custom-call | flops 452984832 | bytes 1179648 | tf_op jit(solution)/shard_map/add_tile/pallas_call | solution.py:50
  36.9 0.0 collective-permute-done.12.refs_6_
  36.9 2.5 %add_tile.5 = (f32[96,512]{1,0:T(8,128)S(1)}, f32[96,512]{1,0:T(8,128)S(1)}) custom-call(s32[4]{0:T(128)S(1)} %pad_add_fusion.2.refs_0_, f32[96,512]{1,0:T(8,128)S(1)} %copy-done, f32[96,512]{1,0:T(8,128)S(1)} %collective-permute-done.refs_2_, f32[96,512]{1,0:T(8,128)S(1)} %collective-permute-done.9.refs_3_, f32[96,512]{1,0:T(8,128)S(1)} %collective-permute-done.10.refs_4_, ...), custom_call_target="tpu_custom_call" | custom-call | flops 452984832 | bytes 1179648 | tf_op jit(solution)/shard_map/add_tile/pallas_call | solution.py:50
  39.4 0.0 collective-permute-done.7.refs_5_
  39.5 0.0 collective-permute-done.8.refs_6_
  39.5 2.4 %add_tile.6 = (f32[96,512]{1,0:T(8,128)S(1)}, f32[96,512]{1,0:T(8,128)S(1)}) custom-call(s32[4]{0:T(128)S(1)} %pad_add_fusion.1.refs_0_, f32[96,512]{1,0:T(8,128)S(1)} %copy-done, f32[96,512]{1,0:T(8,128)S(1)} %collective-permute-done.refs_2_, f32[96,512]{1,0:T(8,128)S(1)} %collective-permute-done.5.refs_3_, f32[96,512]{1,0:T(8,128)} %collective-permute-done.6.refs_4_, ...), custom_call_target="tpu_custom_call" | custom-call | flops 452984832 | bytes 1179648 | tf_op jit(solution)/shard_map/add_tile/pallas_call | solution.py:50
  41.9 0.0 collective-permute-done.3.refs_5_
  41.9 0.0 collective-permute-done.4.refs_6_
  41.9 2.0 %add_tile.7 = (f32[96,512]{1,0:T(8,128)S(1)}, f32[96,512]{1,0:T(8,128)S(1)}) custom-call(s32[4]{0:T(128)S(1)} %pad_add_fusion.refs_0_, f32[96,512]{1,0:T(8,128)S(1)} %copy-done, f32[96,512]{1,0:T(8,128)S(1)} %collective-permute-done.refs_2_, f32[96,512]{1,0:T(8,128)S(1)} %collective-permute-done.1.refs_3_, f32[96,512]{1,0:T(8,128)S(1)} %collective-permute-done.2.refs_4_, ...), custom_call_target="tpu_custom_call" | custom-call | flops 452984832 | bytes 1179648 | tf_op jit(solution)/shard_map/add_tile/pallas_call | solution.py:50
  44.0 0.1 collective-permute-start.16
  44.1 1.4 %collective-permute-done.16 = f32[96,512]{1,0:T(8,128)S(1)} collective-permute-done((f32[96,512]{1,0:T(8,128)S(1)}, f32[96,512]{1,0:T(8,128)S(1)}, u32[]{:S(2)}, u32[]{:S(2)}) %collective-permute-start.16) | collective-permute-done | bytes 196640 | tf_op jit(solution)/shard_map/ppermute | solution.py:72
  45.5 0.7 %add.29 = f32[96,512]{1,0:T(8,128)} add(f32[96,512]{1,0:T(8,128)S(1)} %get-tuple-element.19, f32[96,512]{1,0:T(8,128)S(1)} %collective-permute-done.16) | non-fusion elementwise | flops 49152 | bytes 589824 | tf_op jit(solution)/shard_map/add | solution.py:101
  (1 shorter events, 0.0 us)
Async XLA Ops:
  0.0 13.1 %collective-permute-start = (f32[96,512]{1,0:T(8,128)}, f32[96,512]{1,0:T(8,128)S(1)}, u32[]{:S(2)}, u32[]{:S(2)}) collective-permute-start(f32[96,512]{1,0:T(8,128)} %refs_1_.7), channel_id=1, source_target_pairs={{0,1},{1,0},{2,3},{3,2},{4,5},{5,4},{6,7},{7,6},{8,9},{9,8},{10,11... | collective-permute-start | bytes 589832 | tf_op jit(solution)/shard_map/ppermute | solution.py:72
  0.5 15.7 %collective-permute-start.13 = (f32[96,512]{1,0:T(8,128)}, f32[96,512]{1,0:T(8,128)S(1)}, u32[]{:S(2)}, u32[]{:S(2)}) collective-permute-start(f32[96,512]{1,0:T(8,128)} %refs_1_.7), channel_id=1, source_target_pairs={{0,2},{1,5},{2,0},{3,7},{4,6},{5,1},{6,4},{7,3},{8,10},{9,13},{10,... | collective-permute-start | bytes 589832 | tf_op jit(solution)/shard_map/ppermute | solution.py:72
  3.0 13.6 %collective-permute-start.14 = (f32[96,512]{1,0:T(8,128)}, f32[96,512]{1,0:T(8,128)S(1)}, u32[]{:S(2)}, u32[]{:S(2)}) collective-permute-start(f32[96,512]{1,0:T(8,128)} %refs_1_.7), channel_id=1, source_target_pairs={{0,4},{1,3},{2,6},{3,1},{4,0},{5,7},{6,2},{7,5},{8,12},{9,11},{10,... | collective-permute-start | bytes 589832 | tf_op jit(solution)/shard_map/ppermute | solution.py:72
  4.5 11.0 %collective-permute-start.9 = (f32[96,512]{1,0:T(8,128)}, f32[96,512]{1,0:T(8,128)S(1)}, u32[]{:S(2)}, u32[]{:S(2)}) collective-permute-start(f32[96,512]{1,0:T(8,128)} %refs_1_.7), channel_id=1, source_target_pairs={{0,8},{1,9},{2,10},{3,11},{4,12},{5,13},{6,14},{7,15},{8,0},{9,1},... | collective-permute-start | bytes 589832 | tf_op jit(solution)/shard_map/ppermute | solution.py:72
  6.1 16.2 %collective-permute-start.5 = (f32[96,512]{1,0:T(8,128)}, f32[96,512]{1,0:T(8,128)S(1)}, u32[]{:S(2)}, u32[]{:S(2)}) collective-permute-start(f32[96,512]{1,0:T(8,128)} %refs_1_.7), channel_id=1, source_target_pairs={{0,16},{1,17},{2,18},{3,19},{4,20},{5,21},{6,22},{7,23},{8,24},{9,... | collective-permute-start | bytes 589832 | tf_op jit(solution)/shard_map/ppermute | solution.py:72
  10.7 2.4 %copy-start = (f32[96,512]{1,0:T(8,128)S(1)}, f32[96,512]{1,0:T(8,128)}, u32[]{:S(2)}) copy-start(f32[96,512]{1,0:T(8,128)} %refs_1_.7) | copy-start | bytes 589828
  13.1 9.7 %collective-permute-start.1 = (f32[96,512]{1,0:T(8,128)S(1)}, f32[96,512]{1,0:T(8,128)S(1)}, u32[]{:S(2)}, u32[]{:S(2)}) collective-permute-start(f32[96,512]{1,0:T(8,128)S(1)} %copy-done), channel_id=1, source_target_pairs={{0,24},{1,25},{2,26},{3,27},{4,28},{5,29},{6,30},{7,31},{8,16},{9,... | collective-permute-start | bytes 589832 | tf_op jit(solution)/shard_map/ppermute | solution.py:72
  15.5 8.8 %collective-permute-start.10 = (f32[96,512]{1,0:T(8,128)S(1)}, f32[96,512]{1,0:T(8,128)S(1)}, u32[]{:S(2)}, u32[]{:S(2)}) collective-permute-start(f32[96,512]{1,0:T(8,128)S(1)} %collective-permute-done.9.refs_3_), channel_id=1, source_target_pairs={{0,2},{1,5},{2,0},{3,7},{4,6},{5,1},{6,4},{7,3},{8,10},{9,13},{10,... | collective-permute-start | bytes 589832 | tf_op jit(solution)/shard_map/ppermute | solution.py:72
  16.2 12.1 %collective-permute-start.11 = (f32[96,512]{1,0:T(8,128)S(1)}, f32[96,512]{1,0:T(8,128)}, u32[]{:S(2)}, u32[]{:S(2)}) collective-permute-start(f32[96,512]{1,0:T(8,128)S(1)} %collective-permute-done.9.refs_3_), channel_id=1, source_target_pairs={{0,4},{1,3},{2,6},{3,1},{4,0},{5,7},{6,2},{7,5},{8,12},{9,11},{10,... | collective-permute-start | bytes 589832 | tf_op jit(solution)/shard_map/ppermute | solution.py:72
  16.5 10.6 %collective-permute-start.15 = (f32[96,512]{1,0:T(8,128)S(1)}, f32[96,512]{1,0:T(8,128)S(1)}, u32[]{:S(2)}, u32[]{:S(2)}) collective-permute-start(f32[96,512]{1,0:T(8,128)S(1)} %collective-permute-done.13.refs_4_), channel_id=1, source_target_pairs={{0,4},{1,3},{2,6},{3,1},{4,0},{5,7},{6,2},{7,5},{8,12},{9,11},{10,... | collective-permute-start | bytes 589832 | tf_op jit(solution)/shard_map/ppermute | solution.py:72
  22.3 7.9 %collective-permute-start.6 = (f32[96,512]{1,0:T(8,128)S(1)}, f32[96,512]{1,0:T(8,128)}, u32[]{:S(2)}, u32[]{:S(2)}) collective-permute-start(f32[96,512]{1,0:T(8,128)S(1)} %collective-permute-done.5.refs_3_), channel_id=1, source_target_pairs={{0,2},{1,5},{2,0},{3,7},{4,6},{5,1},{6,4},{7,3},{8,10},{9,13},{10,... | collective-permute-start | bytes 589832 | tf_op jit(solution)/shard_map/ppermute | solution.py:72
  22.8 11.4 %collective-permute-start.2 = (f32[96,512]{1,0:T(8,128)S(1)}, f32[96,512]{1,0:T(8,128)S(1)}, u32[]{:S(2)}, u32[]{:S(2)}) collective-permute-start(f32[96,512]{1,0:T(8,128)S(1)} %collective-permute-done.1.refs_3_), channel_id=1, source_target_pairs={{0,2},{1,5},{2,0},{3,7},{4,6},{5,1},{6,4},{7,3},{8,10},{9,13},{10,... | collective-permute-start | bytes 589832 | tf_op jit(solution)/shard_map/ppermute | solution.py:72
  24.4 12.5 %collective-permute-start.12 = (f32[96,512]{1,0:T(8,128)S(1)}, f32[96,512]{1,0:T(8,128)}, u32[]{:S(2)}, u32[]{:S(2)}) collective-permute-start(f32[96,512]{1,0:T(8,128)S(1)} %collective-permute-done.10.refs_4_), channel_id=1, source_target_pairs={{0,4},{1,3},{2,6},{3,1},{4,0},{5,7},{6,2},{7,5},{8,12},{9,11},{10,... | collective-permute-start | bytes 589832 | tf_op jit(solution)/shard_map/ppermute | solution.py:72
  27.1 12.3 %collective-permute-start.7 = (f32[96,512]{1,0:T(8,128)S(1)}, f32[96,512]{1,0:T(8,128)S(1)}, u32[]{:S(2)}, u32[]{:S(2)}) collective-permute-start(f32[96,512]{1,0:T(8,128)S(1)} %collective-permute-done.5.refs_3_), channel_id=1, source_target_pairs={{0,4},{1,3},{2,6},{3,1},{4,0},{5,7},{6,2},{7,5},{8,12},{9,11},{10,... | collective-permute-start | bytes 589832 | tf_op jit(solution)/shard_map/ppermute | solution.py:72
  28.3 13.6 %collective-permute-start.3 = (f32[96,512]{1,0:T(8,128)S(1)}, f32[96,512]{1,0:T(8,128)S(1)}, u32[]{:S(2)}, u32[]{:S(2)}) collective-permute-start(f32[96,512]{1,0:T(8,128)S(1)} %collective-permute-done.1.refs_3_), channel_id=1, source_target_pairs={{0,4},{1,3},{2,6},{3,1},{4,0},{5,7},{6,2},{7,5},{8,12},{9,11},{10,... | collective-permute-start | bytes 589832 | tf_op jit(solution)/shard_map/ppermute | solution.py:72
  30.2 9.3 %collective-permute-start.8 = (f32[96,512]{1,0:T(8,128)}, f32[96,512]{1,0:T(8,128)S(1)}, u32[]{:S(2)}, u32[]{:S(2)}) collective-permute-start(f32[96,512]{1,0:T(8,128)} %collective-permute-done.6.refs_4_), channel_id=1, source_target_pairs={{0,4},{1,3},{2,6},{3,1},{4,0},{5,7},{6,2},{7,5},{8,12},{9,11},{10,... | collective-permute-start | bytes 589832 | tf_op jit(solution)/shard_map/ppermute | solution.py:72
  34.3 7.7 %collective-permute-start.4 = (f32[96,512]{1,0:T(8,128)S(1)}, f32[96,512]{1,0:T(8,128)S(1)}, u32[]{:S(2)}, u32[]{:S(2)}) collective-permute-start(f32[96,512]{1,0:T(8,128)S(1)} %collective-permute-done.2.refs_4_), channel_id=1, source_target_pairs={{0,4},{1,3},{2,6},{3,1},{4,0},{5,7},{6,2},{7,5},{8,12},{9,11},{10,... | collective-permute-start | bytes 589832 | tf_op jit(solution)/shard_map/ppermute | solution.py:72
  44.0 1.5 %collective-permute-start.16 = (f32[96,512]{1,0:T(8,128)S(1)}, f32[96,512]{1,0:T(8,128)S(1)}, u32[]{:S(2)}, u32[]{:S(2)}) collective-permute-start(f32[96,512]{1,0:T(8,128)S(1)} %get-tuple-element.20), channel_id=1, source_target_pairs={{0,1},{1,0},{2,3},{3,2},{4,5},{5,4},{6,7},{7,6},{8,9},{9,8},{10,11... | collective-permute-start | bytes 589832 | tf_op jit(solution)/shard_map/ppermute | solution.py:72
